TPU v7x, 32 devices: a whole 2x2x4 slice. The times are simulated.
32 devices in a mesh: row: 8 (over z, x), col: 4 (over y, core).
Axes of the slice: x: 2, y: 2, z: 4, core: 2. Of those that a mesh axis runs over, the one named last changes fastest.
Arguments:
- gradients: bfloat16 [32, 2, 524288], P(('row', 'col')), may hold values from -96 to 96
- master_params: float32 [2, 524288], P(None, ('row', 'col')), may hold values from -0.1 to 0.1
- first_moment: float32 [2, 524288], P(None, ('row', 'col')), may hold values from -3 to 3
- second_moment: float32 [2, 524288], P(None, ('row', 'col')), may hold values from 0.05 to 5
Outputs:
- new_master: float32 [2, 524288], P(None, ('row', 'col'))
- new_first: float32 [2, 524288], P(None, ('row', 'col'))
- new_second: float32 [2, 524288], P(None, ('row', 'col'))
- new_weights: bfloat16 [2, 524288], replicated
All inputs are finite; a program needn't handle non-finite values.
Results may differ from a plain program's by a relative error of at most 0.009.
Values may be sent and summed in bfloat16 or wider, within the bound.
A program may use at most 64 MiB of HBM per device.

v0:
```python
import functools

import jax
import jax.numpy as jnp
import numpy as np
from jax import lax
from jax.experimental import pallas as pl
from jax.experimental.pallas import tpu as pltpu
from jax.sharding import PartitionSpec as P

beta_one = 0.9
beta_two = 0.95
learn_rate = 0.001
decay_rate = 0.1
epsilon = 1e-08
adam_step = 10.0

LANES = 128
SPLIT = ((56, "x"), (56, "y"), (48, "x"), (48, "y"), (48, "z"))
STEP_ROWS = 8
VMEM_LIMIT = 40 * 1024 * 1024
MESH = pl.DeviceIdType.MESH


def adam_update(mean_grad, master_params, first_moment, second_moment):
    new_first = beta_one * first_moment + (1.0 - beta_one) * mean_grad
    new_second = beta_two * second_moment + (1.0 - beta_two) * mean_grad * mean_grad
    first_hat = new_first / (1.0 - beta_one**adam_step)
    second_hat = new_second / (1.0 - beta_two**adam_step)
    new_master = master_params - learn_rate * (
        first_hat / (jnp.sqrt(second_hat) + epsilon) + decay_rate * master_params
    )
    return (new_master, new_first, new_second)


def factors(n):
    out = []
    while n > 1:
        k = next(k for k in (4, 2, *range(3, n + 1)) if n % k == 0)
        out.append(k)
        n //= k
    return out


def digits_of(rows, cols):
    core = [2] if cols % 2 == 0 else []
    found = []
    for axis, sizes in (("row", factors(rows)), ("col", factors(cols // (2 if core else 1)) + core)):
        stride = int(np.prod(sizes, dtype=np.int64))
        for size in sizes:
            stride //= size
            found.append((axis, size, stride))
    return found


def orders_of(digits):
    last = len(digits) - 1
    row_at = [i for i in range(last) if digits[i][0] == "row"]
    col_at = [i for i in range(last) if digits[i][0] == "col"]
    x, y = row_at[-1:], col_at[:1]
    rest = col_at[1:] + row_at[:-1]
    return {"x": [last] + x + y + rest, "y": [last] + y + x + rest, "z": [last] + rest + x + y, "w": [last] + rest + y + x}


def kernel(digits, flow_orders, rows, grad, master, first, second, new_master, new_first, new_second, weights, scratch):
    count = len(digits)
    devices = int(np.prod([d[1] for d in digits]))
    at = {axis: lax.axis_index(axis) for axis in ("row", "col")}
    mine = [lax.rem(at[axis] // stride, size) for axis, size, stride in digits]

    def peer(digit, t):
        axis, size, stride = digits[digit]
        value = lax.rem(mine[digit] + t, size)
        ids = dict(at)
        ids[axis] = at[axis] + (value - mine[digit]) * stride
        return value, (ids["row"], ids["col"])

    flows = len(flow_orders)

    loads = {}
    for keep in (0, 1):
        for f in range(flows):
            digit = flow_orders[f][0]
            for t in [0] if keep else range(1, digits[digit][1]):
                value = peer(digit, t)[0]
                where = tuple(value if i == digit else slice(None) for i in range(count)) + (rows[f],)
                loads[f, t] = pltpu.make_async_copy(
                    grad.at[where], scratch[f"raw{f}"].at[t], scratch["load_sem"].at[f, t]
                )
                loads[f, t].start()
    states = []
    for i, (src, name) in enumerate(((master, "master"), (first, "first"), (second, "second"))):
        copy = pltpu.make_async_copy(src, scratch[name], scratch["state_sem"].at[i])
        copy.start()
        states.append(copy)

    barrier = pltpu.get_barrier_semaphore()
    greeted = 0
    for digit in range(count):
        for t in range(1, digits[digit][1]):
            pl.semaphore_signal(barrier, inc=1, device_id=peer(digit, t)[1], device_id_type=MESH)
            greeted += 1
    pl.semaphore_wait(barrier, greeted)

    sent = []
    pending = {}

    def send(f, step, digit, t, src, dst, device):
        copy = pltpu.make_async_remote_copy(
            src_ref=src,
            dst_ref=dst,
            send_sem=scratch["send_sem"].at[f, step, t - 1],
            recv_sem=scratch["recv_sem"].at[f, step, t - 1],
            device_id=device,
            device_id_type=MESH,
        )
        copy.start()
        sent.append(copy)
        pending.setdefault((f, step), []).append(copy)

    def total(f, p, place):
        order = flow_orders[f]
        value = scratch[f"raw{f}"][(0,) + tuple(place.get(i, mine[i]) for i in sorted(order[1:]))].astype(jnp.float32)
        for q in range(p):
            after = tuple(place.get(i, mine[i]) for i in sorted(order[q + 1 :]))
            for t in range(digits[order[q]][1] - 1):
                value += scratch[f"got{f}_{q}"][(t,) + after].astype(jnp.float32)
        return value

    def scatter(f, p):
        digit = flow_orders[f][p]
        after = sorted(flow_orders[f][p + 1 :])
        for t in range(1, digits[digit][1]):
            value, device = peer(digit, t)
            if p == 0:
                loads[f, t].wait()
                src = scratch[f"raw{f}"].at[t]
            else:
                src = scratch[f"sum{f}_{p}"].at[t - 1]
                for idx in np.ndindex(*(digits[i][1] for i in after)):
                    place = dict(zip(after, idx))
                    place[digit] = value
                    src[idx] = total(f, p, place).astype(jnp.bfloat16)
            send(f, p, digit, t, src, scratch[f"got{f}_{p}"].at[t - 1], device)

    def gather(f, p):
        digit = flow_orders[f][p]
        have = set(flow_orders[f][p + 1 :])
        where = tuple(slice(None) if i in have else mine[i] for i in range(count)) + (rows[f],)
        for t in range(1, digits[digit][1]):
            send(f, 2 * count - 1 - p, digit, t, weights.at[where], weights.at[where], peer(digit, t)[1])

    def arrived(f, step):
        for copy in pending[(f, step)]:
            copy.wait_recv()

    for f in range(flows):
        scatter(f, 0)
    def update(f):
        if f == 0:
            for copy in states:
                copy.wait()
        updated, moment, variance = adam_update(
            total(f, count, {}) / devices,
            scratch["master"][rows[f], :],
            scratch["first"][rows[f], :],
            scratch["second"][rows[f], :],
        )
        weights[tuple(mine) + (rows[f],)] = updated.astype(jnp.bfloat16)
        gather(f, count - 1)
        new_master[rows[f], :] = updated
        new_first[rows[f], :] = moment
        new_second[rows[f], :] = variance

    turns = [(step, f) for step in range(2 * count) for f in range(flows)]
    for step, f in turns:
        if step == 0:
            loads[f, 0].wait()
        arrived(f, step)
        if step < count - 1:
            scatter(f, step + 1)
        elif step == count - 1:
            update(f)
        elif step < 2 * count - 1:
            gather(f, 2 * count - 2 - step)
    for copy in sent:
        copy.wait_send()


def to_rows(x):
    layers, length = x.shape
    return x.reshape(layers, length // LANES, LANES).transpose(1, 0, 2).reshape(layers * length // LANES, LANES)


def from_rows(x, layers):
    total = x.shape[0]
    return x.reshape(total // layers, layers, LANES).transpose(1, 0, 2).reshape(layers, total // layers * LANES)


def write_out(*arrays):
    count = len(arrays)

    def body(*refs):
        copies = [pltpu.make_async_copy(refs[i], refs[count + i], refs[-1].at[i]) for i in range(count)]
        for copy in copies[::-1]:
            copy.start()
        for copy in copies:
            copy.wait()

    return pl.pallas_call(
        body,
        name="write_out",
        out_shape=tuple(jax.ShapeDtypeStruct(x.shape, x.dtype) for x in arrays),
        in_specs=[pl.BlockSpec(memory_space=pltpu.VMEM)] * count,
        out_specs=(pl.BlockSpec(memory_space=pltpu.HBM),) * count,
        scratch_shapes=[pltpu.SemaphoreType.DMA((count,))],
        compiler_params=pltpu.CompilerParams(vmem_limit_bytes=1 << 20),
    )(*arrays)


def shards(digits, gradients, master_params, first_moment, second_moment):
    count = len(digits)
    sizes = tuple(d[1] for d in digits)
    devices = int(np.prod(sizes))
    layers = gradients.shape[1]
    grad = to_rows(gradients[0])
    block = grad.shape[0] // devices
    orders = orders_of(digits)
    whole, start, done = sum(share for share, _ in SPLIT), 0, 0
    flow_orders, rows = [], []
    for share, name in SPLIT:
        done += share
        end = block if done == whole else done * block // whole // STEP_ROWS * STEP_ROWS
        if end > start:
            flow_orders.append(orders[name])
            rows.append(pl.ds(start, end - start))
            start = end
    flows = len(rows)

    most = max(sizes) - 1
    scratch = {
        "load_sem": pltpu.SemaphoreType.DMA((flows, most + 1)),
        "state_sem": pltpu.SemaphoreType.DMA((3,)),
        "send_sem": pltpu.SemaphoreType.DMA((flows, 2 * count, most)),
        "recv_sem": pltpu.SemaphoreType.DMA((flows, 2 * count, most)),
    }
    for name in ("master", "first", "second"):
        scratch[name] = pltpu.VMEM((block, LANES), jnp.float32)
    for f, order in enumerate(flow_orders):
        for p in range(count):
            after = tuple(sizes[i] for i in sorted(order[p + 1 :])) + (rows[f].size, LANES)
            if p == 0:
                scratch[f"raw{f}"] = pltpu.VMEM((sizes[order[p]],) + after, jnp.bfloat16)
            else:
                scratch[f"sum{f}_{p}"] = pltpu.VMEM((sizes[order[p]] - 1,) + after, jnp.bfloat16)
            scratch[f"got{f}_{p}"] = pltpu.VMEM((sizes[order[p]] - 1,) + after, jnp.bfloat16)

    hbm_spec = pl.BlockSpec(memory_space=pltpu.HBM)
    vmem_spec = pl.BlockSpec(memory_space=pltpu.VMEM)
    part = jax.ShapeDtypeStruct((block, LANES), jnp.float32)
    names = list(scratch)

    def body(*refs):
        kernel(digits, flow_orders, rows, *refs[:8], dict(zip(names, refs[8:])))

    new_master, new_first, new_second, weights = pl.pallas_call(
        body,
        name="average_update",
        out_shape=(part, part, part, jax.ShapeDtypeStruct(sizes + (block, LANES), jnp.bfloat16)),
        in_specs=[hbm_spec] * 4,
        out_specs=(vmem_spec,) * 4,
        scratch_shapes=[scratch[name] for name in names],
        compiler_params=pltpu.CompilerParams(
            collective_id=0, has_side_effects=True, vmem_limit_bytes=VMEM_LIMIT
        ),
    )(
        *(
            pltpu.with_memory_space_constraint(x, pltpu.HBM)
            for x in (
                grad.reshape(sizes + (block, LANES)),
                to_rows(master_params),
                to_rows(first_moment),
                to_rows(second_moment),
            )
        )
    )
    results = write_out(new_master, new_first, new_second, weights.reshape(devices * block, LANES))
    return tuple(from_rows(x, layers) for x in results)


def solution(mesh):
    digits = digits_of(mesh.shape["row"], mesh.shape["col"])
    in_specs = (
        P(("row", "col"), None, None),
        P(None, ("row", "col")),
        P(None, ("row", "col")),
        P(None, ("row", "col")),
    )
    out_specs = (P(None, ("row", "col")), P(None, ("row", "col")), P(None, ("row", "col")), P())
    return jax.shard_map(
        functools.partial(shards, digits), mesh=mesh, in_specs=in_specs, out_specs=out_specs, check_vma=False
    )
```

profile of v0, /device:TPU:0, one launch (start us, length us, event | category | flops | bytes accessed | tf_op | source)
XLA Modules:
  0.0 40.0 jit_solution(9543809625517997762)
XLA Ops:
  0.6 37.9 %average_update.1 = (f32[256,128]{1,0:T(8,128)S(1)}, f32[256,128]{1,0:T(8,128)S(1)}, f32[256,128]{1,0:T(8,128)S(1)}, bf16[4,2,2,2,256,128]{5,4,3,2,1,0:T(8,128)(2,1)S(1)}) custom-call(bf16[4,2,2,2,256,128]{5,4,3,2,1,0:T(8,128)(2,1)} %bitcast.42, f32[256,128]{1,0:T(8,128)} %bitcast.43, f32[256,128]{1,0:T(8,128)} %bitcast.44, f32[256,128]{1,0:T(8,128)} %bitcast.45), custom_call_target="tpu_custom_call" | custom-call | tf_op jit(solution)/shard_map/average_update/pallas_call | solution.py:266
  38.5 1.5 %write_out.1 = (f32[256,128]{1,0:T(8,128)}, f32[256,128]{1,0:T(8,128)}, f32[256,128]{1,0:T(8,128)}, bf16[8192,128]{1,0:T(8,128)(2,1)}) custom-call(f32[256,128]{1,0:T(8,128)S(1)} %get-tuple-element.12.refs_0_, f32[256,128]{1,0:T(8,128)S(1)} %get-tuple-element.13.refs_1_, f32[256,128]{1,0:T(8,128)S(1)} %get-tuple-element.14.refs_2_, ...), custom_call_target="tpu_custom_call" | custom-call | tf_op jit(solution)/shard_map/write_out/pallas_call | solution.py:210
where the time goes:
time: 40.1 us; the launch traced here: 40 us
  Pallas kernels  39.3 us (98%)
  between operations  0.64 us (2%)
    pallas_call x1, Pallas kernels, shards(): pl.pallas_call(body, name='average_update', out_shape=(part, part, part,...  37.9 us
    pallas_call x1, Pallas kernels, write_out(): pl.pallas_call(body, name='write_out', out_shape=tuple((jax.ShapeDtypeStr...  1.47 us

commit v1 on v0

v1 whole, which is shorter than its diff:
```python
import functools
import heapq

import jax
import jax.numpy as jnp
import numpy as np
from jax import lax
from jax.experimental import pallas as pl
from jax.experimental.pallas import tpu as pltpu
from jax.sharding import PartitionSpec as P

beta_one = 0.9
beta_two = 0.95
learn_rate = 0.001
decay_rate = 0.1
epsilon = 1e-08
adam_step = 10.0

LANES = 128
FLOWS = ((32, "xyz", "zyx"), (32, "yxz", "yxz"), (24, "zyx", "zxy"), (32, "zyx", "zxy"), (24, "xyz", "zyx"), (40, "xyz", "zxy"), (32, "yzx", "yzx"), (8, "xyz", "zyx"), (8, "xyz", "xyz"), (24, "xyz", "zxy"))
FIRST = (7.2, 103.1, 65.1, -21.2, 31.4, 17.8, 17.5, 33.2, 70.7, 62.1)
STAGE = {('r', 1, 'far'): -116.4, ('r', 1, 'near'): 33.5, ('r', 2, 'far'): -41.5, ('r', 2, 'near'): 1.4, ('r', 2, 'all'): -109.3, ('r', 1, 'all'): -2.1, ('r', 3, 'all'): -41.2, ('g', -1, 0): -37.9, ('g', -1, 1): 89.8, ('g', 0, 1): 0.7, ('g', -1, 2): 82.8, ('g', 0, 2): -7.7, ('g', 1, 2): 16.8, ('g', -1, 3): -21.5, ('g', 0, 3): 76.6, ('g', 1, 3): -54.4, ('g', 2, 3): -60.5}
STEP_ROWS = 8
VMEM_LIMIT = 40 * 1024 * 1024
MESH = pl.DeviceIdType.MESH
CORE_RATE, CORE_LATENCY = 680e3, 1.0
LINK_RATE, LINK_LATENCY, HOP_LATENCY = 46.6e3, 2.2, 0.8
AHEAD = 0.3
STEP = 0.05


def adam_update(mean_grad, master_params, first_moment, second_moment):
    new_first = beta_one * first_moment + (1.0 - beta_one) * mean_grad
    new_second = beta_two * second_moment + (1.0 - beta_two) * mean_grad * mean_grad
    first_hat = new_first / (1.0 - beta_one**adam_step)
    second_hat = new_second / (1.0 - beta_two**adam_step)
    new_master = master_params - learn_rate * (
        first_hat / (jnp.sqrt(second_hat) + epsilon) + decay_rate * master_params
    )
    return (new_master, new_first, new_second)


def factors(n):
    out = []
    while n > 1:
        k = next(k for k in (4, 2, *range(3, n + 1)) if n % k == 0)
        out.append(k)
        n //= k
    return out


def digits_of(rows, cols):
    core = [2] if cols % 2 == 0 else []
    found = []
    for axis, sizes in (("row", factors(rows)), ("col", factors(cols // (2 if core else 1)) + core)):
        stride = int(np.prod(sizes, dtype=np.int64))
        for size in sizes:
            stride //= size
            found.append((axis, size, stride))
    return found


def order_of(digits, name):
    last = len(digits) - 1
    row_at = [i for i in range(last) if digits[i][0] == "row"]
    col_at = [i for i in range(last) if digits[i][0] == "col"]
    groups = {"x": row_at[-1:], "y": col_at[:1], "z": col_at[1:] + row_at[:-1]}
    return [i for letter in name for i in groups[letter]]


class Plan:
    def __init__(self, sizes, flows, first, stage_rank):
        self.sizes, self.flows, self.count = sizes, flows, len(sizes)
        self.first, self.stage_rank = first, stage_rank
        self.messages = {}
        self.build()
        self.simulate()

    def parts(self, f, p):
        order = self.flows[f][0]
        if 0 < p < self.count - 1 and self.sizes[order[p + 1]] == 2:
            return ("far", "near")
        return ("all",)

    def gather_unit(self, f, source, s):
        return ("g", f, s, source if s == 1 else None)

    def rank(self, key):
        f = key[1]
        if key[0] == "r":
            return self.first[f % len(self.first)] + self.stage_rank.get(("r", key[2], key[3]), 0.0)
        return self.first[f % len(self.first)] + self.stage_rank.get(("g", key[2], key[3]), 0.0)

    def cost(self, digit, size_bytes):
        size = self.sizes[digit]
        if digit == self.count - 1:
            return size_bytes * (size - 1) / CORE_RATE, CORE_LATENCY
        lanes = (size // 2) * (size - size // 2)
        return size_bytes * lanes / LINK_RATE, LINK_LATENCY + HOP_LATENCY * (size - 2)

    def build(self):
        sizes, count = self.sizes, self.count
        blocks = lambda digits: int(np.prod([sizes[i] for i in digits], dtype=np.int64))
        for f, (down, up, rows) in enumerate(self.flows):
            for p in range(count):
                parts = self.parts(f, p)
                for part in parts:
                    needs = set()
                    for q in range(p):
                        back = self.parts(f, q)
                        needs.add(("r", f, q, back[0] if q == p - 1 else back[-1]))
                    self.messages["r", f, p, part] = (
                        down[p], blocks(down[p + 1 :]) // len(parts) * rows, needs, ("r", f, p, part)
                    )
            for s in range(count):
                for k in range(-1, s):
                    held = 1 if k < 0 else (sizes[up[k]] - 1) * blocks(up[:k])
                    needs = {("u", f)} if k < 0 else {self.gather_unit(f, j, k) for j in range(-1, k)}
                    if k >= 0:
                        needs = set(needs)
                    self.messages["g", f, k, s] = (up[s], held * rows, needs, self.gather_unit(f, k, s))

    def simulate(self):
        waiting = {key: set(message[2]) for key, message in self.messages.items()}
        users = {}
        for key, needs in waiting.items():
            for unit in needs:
                users.setdefault(unit, []).append(key)
        coming = {}
        for key, message in self.messages.items():
            coming[message[3]] = coming.get(message[3], 0) + 1
        sums = {f: {u for u in coming if u[0] == "r" and u[1] == f} for f in range(len(self.flows))}
        free, events, pending, lands = {}, [], [], {}
        self.actions = []
        serial = 0
        clock = 0.0

        def ready(key):
            heapq.heappush(pending, (self.rank(key), key[1], self.serials[key], key))

        self.serials = {key: i for i, key in enumerate(self.messages)}
        for key, needs in waiting.items():
            if not needs:
                ready(key)

        def dispatch():
            nonlocal serial
            again = []
            while pending:
                item = heapq.heappop(pending)
                key = item[3]
                digit, amount, _, unit = self.messages[key]
                if free.get(digit, 0.0) > clock + AHEAD:
                    again.append(item)
                    continue
                took, latency = self.cost(digit, amount * LANES * 2)
                free[digit] = max(clock, free.get(digit, 0.0)) + took
                self.actions.append(("send",) + key)
                lands[unit] = max(lands.get(unit, 0.0), free[digit] + latency)
                coming[unit] -= 1
                serial += 1
                if coming[unit] == 0:
                    heapq.heappush(events, (lands[unit], serial, unit))
                else:
                    heapq.heappush(events, (free[digit], serial, None))
                serial += 1
                heapq.heappush(events, (max(clock, free[digit] - AHEAD), serial, None))
            for item in again:
                heapq.heappush(pending, item)

        def arrive(unit):
            nonlocal clock
            f = unit[1]
            for key in users.get(unit, ()):
                waiting[key].discard(unit)
                if not waiting[key]:
                    ready(key)
            if unit[0] == "r":
                sums[f].discard(unit)
                if not sums[f]:
                    self.actions.append(("update", f))
                    clock += 0.1
                    arrive(("u", f))
                    self.actions.append(("store", f))

        dispatch()
        while events:
            at, _, unit = heapq.heappop(events)
            clock = max(clock, at)
            if unit is not None:
                self.actions.append(("wait",) + unit)
                clock += STEP
                arrive(unit)
            dispatch()
        assert not pending
        self.finish = clock


def kernel(digits, plan, rows, flat, grad, master, first, second, new_master, new_first, new_second, weights, scratch):
    sizes, count = plan.sizes, plan.count
    devices = int(np.prod(sizes))
    core = count - 1
    at = {axis: lax.axis_index(axis) for axis in ("row", "col")}
    mine = [lax.rem(at[axis] // stride, size) for axis, size, stride in digits]

    def peer(digit, t):
        axis, size, stride = digits[digit]
        value = lax.rem(mine[digit] + t, size)
        ids = dict(at)
        ids[axis] = at[axis] + (value - mine[digit]) * stride
        return value, (ids["row"], ids["col"])

    raw = scratch["raw"]
    for t in range(sizes[core] - 1, -1, -1):
        for i in range(sizes[0]):
            where = (i,) + (slice(None),) * (count - 2) + (peer(core, t)[0],)
            pltpu.make_async_copy(grad.at[where], raw.at[t, i], scratch["load_sem"].at[t]).start()
    for i, src in enumerate((master, first, second)):
        pltpu.make_async_copy(src, scratch["state"].at[i], scratch["load_sem"].at[sizes[core]]).start()

    barrier = pltpu.get_barrier_semaphore()
    greeted = 0
    for digit in range(count):
        for t in range(1, sizes[digit]):
            pl.semaphore_signal(barrier, inc=1, device_id=peer(digit, t)[1], device_id_type=MESH)
            greeted += 1
    pl.semaphore_wait(barrier, greeted)

    def loaded(t):
        ref = scratch["state"] if t == sizes[core] else raw.at[t]
        pltpu.make_async_copy(ref, ref, scratch["load_sem"].at[t]).wait()

    for t in range(sizes[core] - 1, -1, -1):
        loaded(t)

    units = {}

    def recv_sem(unit):
        return scratch["recv_sem"].at[units.setdefault(unit, len(units))]

    def send(phase, unit, src, dst, device):
        pltpu.make_async_remote_copy(
            src_ref=src,
            dst_ref=dst,
            send_sem=scratch["send_sem"].at[phase],
            recv_sem=recv_sem(unit),
            device_id=device,
            device_id_type=MESH,
        ).start()

    def wait(unit, ref):
        pltpu.make_async_remote_copy(
            src_ref=ref,
            dst_ref=ref,
            send_sem=scratch["send_sem"].at[0],
            recv_sem=recv_sem(unit),
            device_id=peer(core, 1)[1],
            device_id_type=MESH,
        ).wait_recv()

    def got_index(f, p, place):
        order = plan.flows[f][0]
        return tuple(place.get(i, mine[i]) for i in sorted(order[p + 1 :]))

    def total(f, p, place):
        order = plan.flows[f][0]
        value = raw[(0,) + tuple(place.get(i, mine[i]) for i in range(core)) + (rows[f],)].astype(jnp.float32)
        for q in range(p):
            for t in range(sizes[order[q]] - 1):
                value += scratch[f"got{f}_{q}"][(t,) + got_index(f, q, place)].astype(jnp.float32)
        return value

    def part_index(f, p, part):
        order = plan.flows[f][0]
        after = sorted(order[p + 1 :])
        if part == "all":
            return tuple(slice(None) for _ in after)
        fixed = peer(order[p + 1], 1 if part == "far" else 0)[0]
        return tuple(fixed if i == order[p + 1] else slice(None) for i in after)

    def scatter(f, p, part):
        order = plan.flows[f][0]
        digit = order[p]
        after = sorted(order[p + 1 :])
        for t in range(1, sizes[digit]):
            value, device = peer(digit, t)
            index = (t - 1,) + part_index(f, p, part)
            if p == 0:
                src = raw.at[(t,) + (slice(None),) * core + (rows[f],)]
            else:
                free = [i for i in after if part == "all" or i != order[p + 1]]
                for idx in np.ndindex(*(sizes[i] for i in free)):
                    place = dict(zip(free, idx))
                    place[digit] = value
                    if part != "all":
                        place[order[p + 1]] = peer(order[p + 1], 1 if part == "far" else 0)[0]
                    slot = (t - 1,) + tuple(place[i] for i in after)
                    scratch[f"sum{f}_{p}"][slot] = total(f, p, place).astype(jnp.bfloat16)
                src = scratch[f"sum{f}_{p}"].at[index]
            send(0, ("r", f, p, part), src, scratch[f"got{f}_{p}"].at[index], device)

    def forward(f, stage, s):
        order = plan.flows[f][1]
        digit = order[s]
        places = [{}]
        if stage >= 0:
            places = [{order[stage]: peer(order[stage], t)[0]} for t in range(1, sizes[order[stage]])]
        for place in places:
            where = tuple(
                slice(None) if i in order[: max(stage, 0)] else place.get(i, mine[i]) for i in range(count)
            ) + (rows[f],)
            for t in range(1, sizes[digit]):
                send(1, plan.gather_unit(f, stage, s), weights.at[where], weights.at[where], peer(digit, t)[1])

    def arrived(unit):
        f = unit[1]
        if unit[0] == "r":
            _, f, p, part = unit
            wait(unit, scratch[f"got{f}_{p}"].at[(slice(None),) + part_index(f, p, part)])
        else:
            _, f, s, source = unit
            order = plan.flows[f][1]
            where = [0] * count
            where[order[s]] = pl.ds(0, sizes[order[s]] - 1)
            for i in order[:s] if source is None else order[: max(source, 0)]:
                where[i] = slice(None)
            if source is not None and source >= 0:
                where[order[source]] = pl.ds(0, sizes[order[source]] - 1)
            wait(unit, weights.at[tuple(where) + (rows[f],)])

    states_ready = False
    results = {}
    for action in plan.actions:
        kind, rest = action[0], action[1:]
        if kind == "wait":
            arrived(rest)
        elif kind == "send":
            (scatter if rest[0] == "r" else forward)(*rest[1:])
        elif kind == "update":
            (f,) = rest
            if not states_ready:
                loaded(sizes[core])
                states_ready = True
            results[f] = adam_update(
                total(f, count, {}) / devices, *(scratch["state"][i, rows[f], :] for i in range(3))
            )
            weights[tuple(mine) + (rows[f],)] = results[f][0].astype(jnp.bfloat16)
        else:
            (f,) = rest
            for ref, value in zip((new_master, new_first, new_second), results.pop(f)):
                ref[rows[f], :] = value
    for phase in range(2):
        ref = flat.at[pl.ds(0, devices - 1)]
        pltpu.make_async_copy(ref, ref, scratch["send_sem"].at[phase]).wait()


def to_rows(x):
    layers, length = x.shape
    return x.reshape(layers, length // LANES, LANES).transpose(1, 0, 2).reshape(layers * length // LANES, LANES)


def from_rows(x, layers):
    total = x.shape[0]
    return x.reshape(total // layers, layers, LANES).transpose(1, 0, 2).reshape(layers, total // layers * LANES)


def write_out(*arrays):
    count = len(arrays)

    def body(*refs):
        copies = [pltpu.make_async_copy(refs[i], refs[count + i], refs[-1].at[i]) for i in range(count)]
        for copy in copies[::-1]:
            copy.start()
        for copy in copies:
            copy.wait()

    return pl.pallas_call(
        body,
        name="write_out",
        out_shape=tuple(jax.ShapeDtypeStruct(x.shape, x.dtype) for x in arrays),
        in_specs=[pl.BlockSpec(memory_space=pltpu.VMEM)] * count,
        out_specs=(pl.BlockSpec(memory_space=pltpu.HBM),) * count,
        scratch_shapes=[pltpu.SemaphoreType.DMA((count,))],
        compiler_params=pltpu.CompilerParams(vmem_limit_bytes=1 << 20),
    )(*arrays)


def shards(digits, gradients, master_params, first_moment, second_moment):
    count = len(digits)
    sizes = tuple(d[1] for d in digits)
    devices = int(np.prod(sizes))
    layers = gradients.shape[1]
    grad = to_rows(gradients[0])
    block = grad.shape[0] // devices
    core = count - 1
    whole, start, done = sum(share for share, _, _ in FLOWS), 0, 0
    flows, rows = [], []
    for share, down, up in FLOWS:
        done += share
        end = block if done == whole else done * block // whole // STEP_ROWS * STEP_ROWS
        if end > start:
            flows.append(([core] + order_of(digits, down), order_of(digits, up) + [core], end - start))
            rows.append(pl.ds(start, end - start))
            start = end
    plan = Plan(sizes, flows, FIRST, STAGE)

    scratch = {
        "load_sem": pltpu.SemaphoreType.DMA((sizes[-1] + 1,)),
        "send_sem": pltpu.SemaphoreType.DMA((2,)),
        "recv_sem": pltpu.SemaphoreType.DMA((sum(a[0] == "wait" for a in plan.actions),)),
        "state": pltpu.VMEM((3, block, LANES), jnp.float32),
        "raw": pltpu.VMEM((sizes[-1],) + sizes[:-1] + (block, LANES), jnp.bfloat16),
    }
    for f, (order, _, count_rows) in enumerate(flows):
        for p in range(count):
            after = tuple(sizes[i] for i in sorted(order[p + 1 :])) + (count_rows, LANES)
            if p > 0:
                scratch[f"sum{f}_{p}"] = pltpu.VMEM((sizes[order[p]] - 1,) + after, jnp.bfloat16)
            scratch[f"got{f}_{p}"] = pltpu.VMEM((sizes[order[p]] - 1,) + after, jnp.bfloat16)

    hbm_spec = pl.BlockSpec(memory_space=pltpu.HBM)
    vmem_spec = pl.BlockSpec(memory_space=pltpu.VMEM)
    part = jax.ShapeDtypeStruct((block, LANES), jnp.float32)
    names = list(scratch)

    def body(*refs):
        kernel(digits, plan, rows, *refs[:9], dict(zip(names, refs[9:])))

    new_master, new_first, new_second, weights = pl.pallas_call(
        body,
        name="average_update",
        out_shape=(part, part, part, jax.ShapeDtypeStruct(sizes + (block, LANES), jnp.bfloat16)),
        in_specs=[hbm_spec] * 5,
        out_specs=(vmem_spec,) * 4,
        scratch_shapes=[scratch[name] for name in names],
        compiler_params=pltpu.CompilerParams(
            collective_id=0, has_side_effects=True, vmem_limit_bytes=VMEM_LIMIT
        ),
    )(
        *(
            pltpu.with_memory_space_constraint(x, pltpu.HBM)
            for x in (
                grad.reshape((devices, block, LANES)),
                grad.reshape(sizes + (block, LANES)),
                to_rows(master_params),
                to_rows(first_moment),
                to_rows(second_moment),
            )
        )
    )
    results = write_out(new_master, new_first, new_second, weights.reshape(devices * block, LANES))
    return tuple(from_rows(x, layers) for x in results)


def solution(mesh):
    digits = digits_of(mesh.shape["row"], mesh.shape["col"])
    in_specs = (
        P(("row", "col"), None, None),
        P(None, ("row", "col")),
        P(None, ("row", "col")),
        P(None, ("row", "col")),
    )
    out_specs = (P(None, ("row", "col")), P(None, ("row", "col")), P(None, ("row", "col")), P())
    return jax.shard_map(
        functools.partial(shards, digits), mesh=mesh, in_specs=in_specs, out_specs=out_specs, check_vma=False
    )
```

time: 40.1 us -> 35.4 us (0.88)
  Pallas kernels: 39.3 us -> 34.6 us
    pallas_call x1, Pallas kernels: 37.9 us -> 33.1 us  [shards(): pl.pallas_call(body, name='average_update', out_shape=(part, part, part,...]
where the time goes in v1:
time: 35.4 us; the launch traced here: 35.3 us
  Pallas kernels  34.6 us (98%)
  between operations  0.64 us (2%)
    pallas_call x1, Pallas kernels, shards(): pl.pallas_call(body, name='average_update', out_shape=(part, part, part,...  33.1 us
    pallas_call x1, Pallas kernels, write_out(): pl.pallas_call(body, name='write_out', out_shape=tuple((jax.ShapeDtypeStr...  1.47 us

profile of v1, /device:TPU:0, one launch (start us, length us, event | category | flops | bytes accessed | tf_op | source)
XLA Modules:
  0.0 35.3 jit_solution(8530180521570972802)
XLA Ops:
  0.6 33.1 %average_update.1 = (f32[256,128]{1,0:T(8,128)S(1)}, f32[256,128]{1,0:T(8,128)S(1)}, f32[256,128]{1,0:T(8,128)S(1)}, bf16[4,2,2,2,256,128]{5,4,3,2,1,0:T(8,128)(2,1)S(1)}) custom-call(bf16[32,256,128]{2,1,0:T(8,128)(2,1)} %bitcast.44, bf16[4,2,2,2,256,128]{5,4,3,2,1,0:T(8,128)(2,1)} %bitcast.45, f32[256,128]{1,0:T(8,128)} %bitcast.46, f32[256,128]{1,0:T(8,128)} %bitcast.47, ...), custom_call_target="tpu_custom_call" | custom-call | tf_op jit(solution)/shard_map/average_update/pallas_call | solution.py:429
  33.8 1.5 %write_out.1 = (f32[256,128]{1,0:T(8,128)}, f32[256,128]{1,0:T(8,128)}, f32[256,128]{1,0:T(8,128)}, bf16[8192,128]{1,0:T(8,128)(2,1)}) custom-call(f32[256,128]{1,0:T(8,128)S(1)} %get-tuple-element.12.refs_0_, f32[256,128]{1,0:T(8,128)S(1)} %get-tuple-element.13.refs_1_, f32[256,128]{1,0:T(8,128)S(1)} %get-tuple-element.14.refs_2_, ...), custom_call_target="tpu_custom_call" | custom-call | tf_op jit(solution)/shard_map/write_out/pallas_call | solution.py:377

commit v2 on v1

v2 whole, which is shorter than its diff:
```python
import functools
import heapq
import itertools

import jax
import jax.numpy as jnp
import numpy as np
from jax import lax
from jax.experimental import pallas as pl
from jax.experimental.pallas import tpu as pltpu
from jax.sharding import PartitionSpec as P

beta_one = 0.9
beta_two = 0.95
learn_rate = 0.001
decay_rate = 0.1
epsilon = 1e-08
adam_step = 10.0

LANES = 128
STEP_ROWS = 8
VMEM_LIMIT = 40 * 1024 * 1024
MESH = pl.DeviceIdType.MESH

FLOWS = (
    (16, "awb", "wz", (693.4, 364.7), (1, 1, 1), 0),
    (16, "yxz", "zw", (630.4, 654.7), (1, 0, 1), 1),
    (16, "wab", "yzx", (923.8, 248.4), (1, 0, 0), 0),
    (32, "yxz", "zw", (861.6, 445.6), (1, 0, 0), 1),
    (24, "xzy", "wba", (1104.1, 56.1), (0, 1, 1), 0),
    (24, "yxz", "zw", (643.2, 405.4), (1, 1, 0), 1),
    (16, "abw", "bwa", (245.7, 411.5), (0, 1, 0), 0),
    (32, "zw", "bwa", (612.6, 45.4), (0, 0, 0), 0),
    (24, "xyz", "zw", (273.2, 227.3), (0, 0, 0), 1),
    (16, "wz", "zw", (-58.2, 40.6), (1, 1, 1), 0),
    (24, "yxz", "zxy", (646.9, 317.3), (1, 0, 0), 0),
    (16, "awb", "wz", (903.8, 397.2), (1, 1, 1), 1),
)
DOWN_RANK = (
    (-257.8, -75.4, -87.6),
    (-198.2, 130.7, -438.3),
    (228.3, 352.9, 365.2),
    (34.2, -353.5, 32.8),
    (260.2, 128.6, -278.8),
    (183.4, 404.6, 16.4),
)
UP_RANK = (
    (4.9, 222.6, 48.8, -180.0, -50.9, -289.6),
    (-98.2, -171.0, 93.8, 44.2, 62.5, -43.2),
    (1.1, 130.9, -63.1, 261.5, 62.2, 292.1),
    (-45.6, -180.1, -151.6, 23.7, -62.6, 216.6),
    (-55.6, -121.9, -85.9, 148.8, 104.4, 184.5),
    (52.0, 107.0, -33.2, -57.9, 133.2, 105.4),
    (-49.2, -73.1, 181.0, -9.3, -56.4, -141.6),
)
RATE = 46.6e3
COST = {
    "x": ({"x": 1}, 2.2),
    "y": ({"y": 1}, 2.2),
    "a": ({"e": 1}, 2.2),
    "b": ({"e": 1, "m": 2}, 3.0),
    "z": ({"e": 3, "m": 4}, 3.8),
    "w": ({"x": 2, "y": 2}, 3.0),
    "c": ({"c": 46.6 / 680}, 1.0),
}
AHEAD, STEP, UPDATE = 0.3, 0.05, 0.1


def adam_update(mean_grad, master_params, first_moment, second_moment):
    new_first = beta_one * first_moment + (1.0 - beta_one) * mean_grad
    new_second = beta_two * second_moment + (1.0 - beta_two) * mean_grad * mean_grad
    first_hat = new_first / (1.0 - beta_one**adam_step)
    second_hat = new_second / (1.0 - beta_two**adam_step)
    new_master = master_params - learn_rate * (
        first_hat / (jnp.sqrt(second_hat) + epsilon) + decay_rate * master_params
    )
    return (new_master, new_first, new_second)


def factors(n):
    out, k = [], 2
    while n > 1:
        while n % k:
            k += 1
        out.append(k)
        n //= k
    return out


def digits_of(rows, cols):
    core = [2] if cols % 2 == 0 else [1]
    found = []
    for axis, sizes in (("row", factors(rows)), ("col", factors(cols // core[0]) + core)):
        stride = int(np.prod(sizes, dtype=np.int64))
        for size in sizes:
            stride //= size
            found.append((axis, size, stride))
    return found


def stages_of(digits):
    core = len(digits) - 1
    row_at = [i for i in range(core) if digits[i][0] == "row"]
    col_at = [i for i in range(core) if digits[i][0] == "col"]
    x, y, b, a = row_at[2:], col_at[:2], row_at[:1], row_at[1:2] + col_at[2:]
    return {"x": x, "y": y, "a": a, "b": b, "z": b + a, "w": x + y, "c": [core]}


class Plan:
    def __init__(self, sizes, groups, flows):
        self.sizes, self.groups, self.flows = sizes, groups, flows
        self.messages = {}
        self.build()
        self.simulate()

    def size(self, letters):
        return int(np.prod([self.sizes[i] for letter in letters for i in self.groups[letter]], dtype=np.int64))

    def parts(self, f, p):
        down = self.flows[f].down
        if 0 < p < len(down) - 1 and self.size(down[p + 1]) == 2 and self.flows[f].split[p]:
            return ("far", "near")
        return ("all",)

    def gather_unit(self, f, k, s):
        return ("g", f, s, k if self.flows[f].fine and 0 < s < len(self.flows[f].up) - 2 else None)

    def build(self):
        for f, flow in enumerate(self.flows):
            down, up = flow.down, flow.up
            for p in range(len(down)):
                parts = self.parts(f, p)
                needs = [("r", f, q, self.parts(f, q)[0 if q == p - 1 else -1]) for q in range(p)]
                for i, part in enumerate(parts):
                    rank = flow.first[0] + DOWN_RANK[p][i if len(parts) > 1 else 2]
                    amount = self.size(down[p + 1 :]) // len(parts) * flow.rows
                    self.messages["r", f, p, part] = (down[p], amount, rank, set(needs), ("r", f, p, part))
            for s in range(len(up)):
                for k in range(-1, s):
                    held = 1 if k < 0 else (self.size(up[k]) - 1) * self.size(up[:k])
                    needs = [("u", f)] if k < 0 else [self.gather_unit(f, j, k) for j in range(-1, k)]
                    rank = flow.first[1] + UP_RANK[k + 1][s]
                    self.messages["g", f, k, s] = (up[s], held * flow.rows, rank, set(needs), self.gather_unit(f, k, s))

    def simulate(self):
        serial = {key: i for i, key in enumerate(self.messages)}
        needs = {key: set(message[3]) for key, message in self.messages.items()}
        users, coming = {}, {}
        self.blocks = {}
        for key, (letter, amount, _, need, unit) in self.messages.items():
            for other in need:
                users.setdefault(other, []).append(key)
            coming[unit] = coming.get(unit, 0) + 1
            self.blocks[unit] = self.blocks.get(unit, 0) + amount // self.flows[key[1]].rows * (self.size(letter) - 1)
        sums = {f: {u for u in coming if u[:2] == ("r", f)} for f in range(len(self.flows))}
        free, lands, events, pending, order = {}, {}, [], [], itertools.count()
        self.actions = []
        clock = 0.0

        def ready(key):
            heapq.heappush(pending, (self.messages[key][2], key[1], serial[key], key))

        def dispatch():
            later = []
            while pending:
                item = heapq.heappop(pending)
                letter, amount, _, _, unit = self.messages[item[3]]
                links, latency = COST[letter]
                if any(free.get(link, 0.0) > clock + AHEAD for link in links):
                    later.append(item)
                    continue
                end = 0.0
                for link, units in links.items():
                    free[link] = max(clock, free.get(link, 0.0)) + amount * units * LANES * 2 / RATE
                    end = max(end, free[link])
                self.actions.append(("send",) + item[3])
                lands[unit] = max(lands.get(unit, 0.0), end + latency)
                coming[unit] -= 1
                if coming[unit] == 0:
                    heapq.heappush(events, (lands[unit], next(order), unit))
                for link in links:
                    heapq.heappush(events, (max(clock, free[link] - AHEAD), next(order), None))
            for item in later:
                heapq.heappush(pending, item)

        def arrive(unit):
            for key in users.get(unit, ()):
                needs[key].discard(unit)
                if not needs[key]:
                    ready(key)

        for key, need in needs.items():
            if not need:
                ready(key)
        dispatch()
        while events:
            at, _, unit = heapq.heappop(events)
            clock = max(clock, at)
            updated = None
            if unit is not None:
                self.actions.append(("wait",) + unit)
                clock += STEP
                arrive(unit)
                f = unit[1]
                if unit[0] == "r":
                    sums[f].discard(unit)
                    if not sums[f]:
                        self.actions.append(("update", f))
                        clock += UPDATE
                        arrive(("u", f))
                        updated = f
            dispatch()
            if updated is not None:
                self.actions.append(("store", updated))
        self.finish = clock


class Flow:
    def __init__(self, down, up, start, rows, first, split, fine):
        self.down, self.up, self.start, self.rows = down, up, start, rows
        self.first, self.split, self.fine = first, split, fine


def kernel(digits, plan, flat, grad, master, first, second, new_master, new_first, new_second, weights, scratch):
    sizes, groups, count = plan.sizes, plan.groups, len(plan.sizes)
    devices = int(np.prod(sizes))
    core = count - 1
    at = {axis: lax.axis_index(axis) for axis in ("row", "col")}
    mine = [lax.rem(at[axis] // stride, size) for axis, size, stride in digits]
    rows = [pl.ds(flow.start, flow.rows) for flow in plan.flows]

    def value(digit, t):
        return lax.rem(mine[digit] + t, sizes[digit]) if t else mine[digit]

    def offsets(letter):
        return list(itertools.product(*(range(sizes[i]) for i in groups[letter])))[1:]

    def place_of(letter, offset):
        return {i: value(i, t) for i, t in zip(groups[letter], offset)}

    def device_of(place):
        ids = dict(at)
        for i, new in place.items():
            axis, _, stride = digits[i]
            ids[axis] = ids[axis] + (new - mine[i]) * stride
        return (ids["row"], ids["col"])

    raw = scratch["raw"]
    for t in range(sizes[core] - 1, -1, -1):
        for i in range(sizes[0]):
            where = (i,) + (slice(None),) * (count - 2) + (value(core, t),)
            pltpu.make_async_copy(grad.at[where], raw.at[t, i], scratch["load_sem"].at[t]).start()
    for i, src in enumerate((master, first, second)):
        pltpu.make_async_copy(src, scratch["state"].at[i], scratch["load_sem"].at[sizes[core]]).start()

    barrier = pltpu.get_barrier_semaphore()
    greeted = {}
    for letter in sorted({letter for flow in plan.flows for letter in flow.down + flow.up}):
        for offset in offsets(letter):
            known = tuple((i, t) for i, t in zip(groups[letter], offset) if t)
            greeted[tuple(sorted(known))] = device_of(place_of(letter, offset))
    for device in greeted.values():
        pl.semaphore_signal(barrier, inc=1, device_id=device, device_id_type=MESH)
    pl.semaphore_wait(barrier, len(greeted))

    def loaded(t):
        ref = scratch["state"] if t == sizes[core] else raw.at[t]
        pltpu.make_async_copy(ref, ref, scratch["load_sem"].at[t]).wait()

    for t in range(sizes[core] - 1, -1, -1):
        loaded(t)

    units = {}

    def recv_sem(unit):
        return scratch["recv_sem"].at[units.setdefault(unit, len(units))]

    def send(phase, unit, src, dst, device):
        pltpu.make_async_remote_copy(
            src_ref=src,
            dst_ref=dst,
            send_sem=scratch["send_sem"].at[phase],
            recv_sem=recv_sem(unit),
            device_id=device,
            device_id_type=MESH,
        ).start()

    def arrived(unit):
        ref = flat.at[pl.ds(0, plan.blocks[unit]), rows[unit[1]]]
        pltpu.make_async_copy(ref, ref, recv_sem(unit)).wait()

    def after(f, p):
        return sorted(i for letter in plan.flows[f].down[p + 1 :] for i in groups[letter])

    def total(f, p, place):
        down = plan.flows[f].down
        found = raw[(0,) + tuple(place.get(i, mine[i]) for i in range(core)) + (rows[f],)].astype(jnp.float32)
        for q in range(p):
            index = tuple(place.get(i, mine[i]) for i in after(f, q))
            for t in range(plan.size(down[q]) - 1):
                found += scratch[f"got{f}_{q}"][(t,) + index].astype(jnp.float32)
        return found

    def scatter(f, p, part):
        down = plan.flows[f].down
        fixed = {}
        if part != "all":
            (digit,) = groups[down[p + 1]]
            fixed = {digit: value(digit, 1 if part == "far" else 0)}
        for slot, offset in enumerate(offsets(down[p])):
            place = place_of(down[p], offset)
            index = (slot,) + tuple(fixed.get(i, slice(None)) for i in after(f, p))
            if p == 0:
                src = raw.at[offset + (slice(None),) * core + (rows[f],)]
            else:
                free = [i for i in after(f, p) if i not in fixed]
                for idx in np.ndindex(*(sizes[i] for i in free)):
                    here = {**place, **fixed, **dict(zip(free, idx))}
                    at_slot = (slot,) + tuple(here[i] for i in after(f, p))
                    scratch[f"sum{f}_{p}"][at_slot] = total(f, p, here).astype(jnp.bfloat16)
                src = scratch[f"sum{f}_{p}"].at[index]
            send(0, ("r", f, p, part), src, scratch[f"got{f}_{p}"].at[index], device_of(place))

    def forward(f, k, s):
        up = plan.flows[f].up
        free = {i: slice(None) for letter in up[: max(k, 0)] for i in groups[letter]}
        places = [{}]
        if k >= 0:
            group = groups[up[k]]
            places = [
                {**free, group[j]: value(group[j], t), **{i: slice(None) for i in group[j + 1 :]}}
                for j in range(len(group))
                for t in range(1, sizes[group[j]])
            ]
        for place in places:
            ref = weights.at[tuple(place.get(i, mine[i]) for i in range(count)) + (rows[f],)]
            for offset in offsets(up[s]):
                send(1, plan.gather_unit(f, k, s), ref, ref, device_of(place_of(up[s], offset)))

    states_ready = False
    results = {}
    for action in plan.actions:
        kind, rest = action[0], action[1:]
        if kind == "wait":
            arrived(rest)
        elif kind == "send":
            (scatter if rest[0] == "r" else forward)(*rest[1:])
        elif kind == "update":
            (f,) = rest
            if not states_ready:
                loaded(sizes[core])
                states_ready = True
            results[f] = adam_update(
                total(f, len(plan.flows[f].down), {}) / devices, *(scratch["state"][i, rows[f], :] for i in range(3))
            )
            weights[tuple(mine) + (rows[f],)] = results[f][0].astype(jnp.bfloat16)
        else:
            (f,) = rest
            for ref, result in zip((new_master, new_first, new_second), results.pop(f)):
                ref[rows[f], :] = result
    for phase in range(2):
        ref = flat.at[pl.ds(0, devices - 1)]
        pltpu.make_async_copy(ref, ref, scratch["send_sem"].at[phase]).wait()


def to_rows(x):
    layers, length = x.shape
    return x.reshape(layers, length // LANES, LANES).transpose(1, 0, 2).reshape(layers * length // LANES, LANES)


def from_rows(x, layers):
    total = x.shape[0]
    return x.reshape(total // layers, layers, LANES).transpose(1, 0, 2).reshape(layers, total // layers * LANES)


def write_out(*arrays):
    count = len(arrays)

    def body(*refs):
        copies = [pltpu.make_async_copy(refs[i], refs[count + i], refs[-1].at[i]) for i in range(count)]
        for copy in copies[::-1]:
            copy.start()
        for copy in copies:
            copy.wait()

    return pl.pallas_call(
        body,
        name="write_out",
        out_shape=tuple(jax.ShapeDtypeStruct(x.shape, x.dtype) for x in arrays),
        in_specs=[pl.BlockSpec(memory_space=pltpu.VMEM)] * count,
        out_specs=(pl.BlockSpec(memory_space=pltpu.HBM),) * count,
        scratch_shapes=[pltpu.SemaphoreType.DMA((count,))],
        compiler_params=pltpu.CompilerParams(vmem_limit_bytes=1 << 20),
    )(*arrays)


def shards(digits, gradients, master_params, first_moment, second_moment):
    sizes = tuple(d[1] for d in digits)
    groups = stages_of(digits)
    devices = int(np.prod(sizes))
    layers = gradients.shape[1]
    grad = to_rows(gradients[0])
    block = grad.shape[0] // devices
    whole, start, done = sum(flow[0] for flow in FLOWS), 0, 0
    flows = []
    for share, down, up, first, split, fine in FLOWS:
        done += share
        end = block if done == whole else done * block // whole // STEP_ROWS * STEP_ROWS
        if end > start:
            down = [letter for letter in "c" + down if groups[letter]]
            up = [letter for letter in up + "c" if groups[letter]]
            flows.append(Flow(down, up, start, end - start, first, (0,) + split, fine))
            start = end
    plan = Plan(sizes, groups, flows)

    scratch = {
        "load_sem": pltpu.SemaphoreType.DMA((sizes[-1] + 1,)),
        "send_sem": pltpu.SemaphoreType.DMA((2,)),
        "recv_sem": pltpu.SemaphoreType.DMA((sum(action[0] == "wait" for action in plan.actions),)),
        "state": pltpu.VMEM((3, block, LANES), jnp.float32),
        "raw": pltpu.VMEM((sizes[-1],) + sizes[:-1] + (block, LANES), jnp.bfloat16),
    }
    for f, flow in enumerate(flows):
        for p, letter in enumerate(flow.down):
            after = sorted(i for other in flow.down[p + 1 :] for i in groups[other])
            shape = (plan.size(letter) - 1,) + tuple(sizes[i] for i in after) + (flow.rows, LANES)
            if p > 0:
                scratch[f"sum{f}_{p}"] = pltpu.VMEM(shape, jnp.bfloat16)
            scratch[f"got{f}_{p}"] = pltpu.VMEM(shape, jnp.bfloat16)

    hbm_spec = pl.BlockSpec(memory_space=pltpu.HBM)
    vmem_spec = pl.BlockSpec(memory_space=pltpu.VMEM)
    part = jax.ShapeDtypeStruct((block, LANES), jnp.float32)
    names = list(scratch)

    def body(*refs):
        kernel(digits, plan, *refs[:9], dict(zip(names, refs[9:])))

    new_master, new_first, new_second, weights = pl.pallas_call(
        body,
        name="average_update",
        out_shape=(part, part, part, jax.ShapeDtypeStruct(sizes + (block, LANES), jnp.bfloat16)),
        in_specs=[hbm_spec] * 5,
        out_specs=(vmem_spec,) * 4,
        scratch_shapes=[scratch[name] for name in names],
        compiler_params=pltpu.CompilerParams(
            collective_id=0, has_side_effects=True, vmem_limit_bytes=VMEM_LIMIT
        ),
    )(
        *(
            pltpu.with_memory_space_constraint(x, pltpu.HBM)
            for x in (
                grad.reshape((devices, block, LANES)),
                grad.reshape(sizes + (block, LANES)),
                to_rows(master_params),
                to_rows(first_moment),
                to_rows(second_moment),
            )
        )
    )
    results = write_out(new_master, new_first, new_second, weights.reshape(devices * block, LANES))
    return tuple(from_rows(x, layers) for x in results)


def solution(mesh):
    digits = digits_of(mesh.shape["row"], mesh.shape["col"])
    in_specs = (
        P(("row", "col"), None, None),
        P(None, ("row", "col")),
        P(None, ("row", "col")),
        P(None, ("row", "col")),
    )
    out_specs = (P(None, ("row", "col")), P(None, ("row", "col")), P(None, ("row", "col")), P())
    return jax.shard_map(
        functools.partial(shards, digits), mesh=mesh, in_specs=in_specs, out_specs=out_specs, check_vma=False
    )
```

time: 35.4 us -> 32.4 us (0.915)
  Pallas kernels: 34.6 us -> 31.6 us
    pallas_call x1, Pallas kernels: 33.1 us -> 30.2 us  [shards(): pl.pallas_call(body, name='average_update', out_shape=(part, part, part,...]
where the time goes in v2:
time: 32.4 us; the launch traced here: 32.3 us
  Pallas kernels  31.6 us (98%)
  between operations  0.64 us (2%)
    pallas_call x1, Pallas kernels, shards(): pl.pallas_call(body, name='average_update', out_shape=(part, part, part,...  30.2 us
    pallas_call x1, Pallas kernels, write_out(): pl.pallas_call(body, name='write_out', out_shape=tuple((jax.ShapeDtypeStr...  1.47 us

profile of v2, /device:TPU:0, one launch (start us, length us, event | category | flops | bytes accessed | tf_op | source)
XLA Modules:
  0.0 32.3 jit_solution(3861013460410850155)
XLA Ops:
  0.6 30.2 %average_update.1 = (f32[256,128]{1,0:T(8,128)S(1)}, f32[256,128]{1,0:T(8,128)S(1)}, f32[256,128]{1,0:T(8,128)S(1)}, bf16[2,2,2,2,2,256,128]{6,5,4,3,2,1,0:T(8,128)(2,1)S(1)}) custom-call(bf16[32,256,128]{2,1,0:T(8,128)(2,1)} %bitcast.44, bf16[2,2,2,2,2,256,128]{6,5,4,3,2,1,0:T(8,128)(2,1)} %bitcast.45, f32[256,128]{1,0:T(8,128)} %bitcast.46, ...), custom_call_target="tpu_custom_call" | custom-call | tf_op jit(solution)/shard_map/average_update/pallas_call | solution.py:439
  30.8 1.5 %write_out.1 = (f32[256,128]{1,0:T(8,128)}, f32[256,128]{1,0:T(8,128)}, f32[256,128]{1,0:T(8,128)}, bf16[8192,128]{1,0:T(8,128)(2,1)}) custom-call(f32[256,128]{1,0:T(8,128)S(1)} %get-tuple-element.12.refs_0_, f32[256,128]{1,0:T(8,128)S(1)} %get-tuple-element.13.refs_1_, f32[256,128]{1,0:T(8,128)S(1)} %get-tuple-element.14.refs_2_, ...), custom_call_target="tpu_custom_call" | custom-call | tf_op jit(solution)/shard_map/write_out/pallas_call | solution.py:386
